TPU v7x, 256 devices: a whole 4x4x8 slice. The times are simulated.
256 devices in a mesh: blk: 16 (over z, y_lo), grp: 16 (over x, y_hi, core).
Axes of the slice: x: 4, y: 4 (y_hi: 2, y_lo: 2; y = y_hi * 2 + y_lo), z: 8, core: 2. Of those that a mesh axis runs over, the one named last changes fastest.
Arguments:
- frames: bfloat16 [16, 4096, 1024], P('grp', 'blk'), may hold values from -16 to 16
- utt_lengths: int32 [8], replicated, may hold values from 1 to 16384, 65536 in all
- attn_gain: float32 [1024], replicated, may hold values from 0.25 to 1.75
- w_qkv: bfloat16 [1024, 3072], P(None, 'grp'), may hold values from -4 to 4
- w_out: bfloat16 [1024, 1024], replicated, may hold values from -0.375 to 0.375
- conv_gain: float32 [1024], replicated, may hold values from 0.25 to 1.75
- w_glu: bfloat16 [1024, 2048], replicated, may hold values from -0.1875 to 0.1875
- w_depth: float32 [31, 1024], replicated, may hold values from -1 to 1
- depth_gain: float32 [1024], replicated, may hold values from 0.25 to 1.75
- w_proj: bfloat16 [1024, 1024], replicated, may hold values from -0.1875 to 0.1875
Outputs:
- block_out: bfloat16 [16, 4096, 1024], P('grp', 'blk')
Inputs may be any that keep to these rules, and one draw needn't show every extreme that they name: `utt_lengths`: they sum to 65536 and the longest is exactly 16384.
All inputs are finite; a program needn't handle non-finite values.
Results may differ from a plain program's by a relative error of at most 0.0095.
Values may be sent and summed in bfloat16 or wider, within the bound.
No kernel may reach another device: no remote copies, remote signals or barrier semaphores. Data moves between devices by JAX's collectives and lax.ppermute only.
A program may use at most 192 MiB of HBM per device.

v0:
```python
import jax
import jax.numpy as jnp
from jax import lax
from jax.sharding import PartitionSpec as P

HEADS = 16
epsilon = 1e-05
big_negative = -1e30


def padded_2(block, sides, width, periodic):
    for axis, dim in sides:
        count = lax.axis_size(axis)
        forward = [(i, i + 1) for i in range(count - 1)]
        if periodic:
            forward.append((count - 1, 0))
        backward = [(target, source) for source, target in forward]
        low = lax.ppermute(
            lax.slice_in_dim(block, block.shape[dim] - width, None, axis=dim), axis, forward
        )
        high = lax.ppermute(lax.slice_in_dim(block, 0, width, axis=dim), axis, backward)
        block = jnp.concatenate([low, block, high], axis=dim)
    return block


def normalize(values, row_gain):
    center = values - jnp.mean(values, axis=-1, keepdims=True)
    spread = jnp.mean(center * center, axis=-1, keepdims=True)
    return center * lax.rsqrt(spread + epsilon) * row_gain


def segment_of(utt_lengths, positions):
    starts = jnp.cumsum(utt_lengths) - utt_lengths
    started = (starts[None, :] <= positions[:, None]).astype(jnp.int32)
    return jnp.sum(started, axis=1) - 1


def body(
    frames, utt_lengths, attn_gain, w_qkv, w_out, conv_gain, w_glu, w_depth, depth_gain, w_proj
):
    frame_rows = frames.shape[1]
    width = frames.shape[2]
    head_count = HEADS
    head_width = width // head_count
    kernel_half = (w_depth.shape[0] - 1) // 2
    score_scale = head_width ** (-0.5)
    blocks = lax.axis_size("blk")
    block_index = lax.axis_index("blk")
    group_index = lax.axis_index("grp")
    window = frame_rows * blocks
    window_start = group_index * window
    first_frame = window_start + block_index * frame_rows
    local_frames = frames[0]
    local_float = local_frames.astype(jnp.float32)
    normed = normalize(local_float, attn_gain).astype(jnp.bfloat16)
    qkv_rows = jnp.dot(
        normed, lax.all_gather(w_qkv, "grp", axis=1, tiled=True), preferred_element_type=jnp.float32
    ).astype(jnp.bfloat16)
    local_seg = segment_of(utt_lengths, first_frame + jnp.arange(frame_rows, dtype=jnp.int32))
    my_heads = lax.all_to_all(qkv_rows, "blk", split_axis=1, concat_axis=0, tiled=True)
    local_heads = head_count // blocks
    qkv_split = my_heads.reshape(window, local_heads, 3, head_width)
    query_all = qkv_split[:, :, 0, :]
    keys_all = qkv_split[:, :, 1, :]
    values_all = qkv_split[:, :, 2, :]
    window_seg = segment_of(utt_lengths, window_start + jnp.arange(window, dtype=jnp.int32))
    query_block = min(512, window)
    block_count = window // query_block

    def attend(block_id):
        block_start = block_id * query_block
        queries = lax.dynamic_slice_in_dim(query_all, block_start, query_block, 0)
        query_seg = lax.dynamic_slice_in_dim(window_seg, block_start, query_block, 0)
        allowed = (query_seg[:, None] == window_seg[None, :])[None]
        scores = (
            jnp.einsum("qhd,khd->hqk", queries, keys_all, preferred_element_type=jnp.float32)
            * score_scale
        )
        row_max = jnp.max(jnp.where(allowed, scores, big_negative), axis=2, keepdims=True)
        weights = jnp.where(allowed, jnp.exp(scores - row_max), 0.0)
        row_total = jnp.sum(weights, axis=2)
        mixed_values = jnp.einsum(
            "hqk,khd->qhd",
            weights.astype(jnp.bfloat16),
            values_all,
            preferred_element_type=jnp.float32,
        )
        normed_values = mixed_values / jnp.transpose(row_total)[:, :, None]
        return normed_values.reshape(query_block, local_heads * head_width).astype(jnp.bfloat16)

    pieces = lax.map(attend, jnp.arange(block_count, dtype=jnp.int32))
    merged_heads = pieces.reshape(window, local_heads * head_width)
    attended = lax.all_to_all(merged_heads, "blk", split_axis=0, concat_axis=1, tiled=True)
    residual = (local_float + jnp.dot(attended, w_out, preferred_element_type=jnp.float32)).astype(
        jnp.bfloat16
    )
    residual = lax.optimization_barrier(residual)
    conv_in = normalize(residual.astype(jnp.float32), conv_gain).astype(jnp.bfloat16)
    projected = jnp.dot(conv_in, w_glu, preferred_element_type=jnp.float32)
    gated = (projected[:, :width] * jax.nn.sigmoid(projected[:, width:])).astype(jnp.bfloat16)
    gated = lax.optimization_barrier(gated)
    padded = padded_2(gated, (("blk", 0),), kernel_half, True)
    left_rim = padded[:kernel_half]
    right_rim = padded[frame_rows + kernel_half :]
    outer_rims = padded_2(jnp.stack([right_rim, left_rim]), (("grp", 0),), 1, False)
    left_edge = jnp.where(block_index == 0, outer_rims[0], left_rim)
    right_edge = jnp.where(block_index == blocks - 1, outer_rims[3], right_rim)
    extended = jnp.concatenate([left_edge, gated, right_edge], axis=0).astype(jnp.float32)
    extended_seg = segment_of(
        utt_lengths,
        first_frame - kernel_half + jnp.arange(frame_rows + 2 * kernel_half, dtype=jnp.int32),
    )
    mixed_conv = jnp.zeros((frame_rows, width), jnp.float32)
    for offset in range(2 * kernel_half + 1):
        same_seg = (extended_seg[offset : offset + frame_rows] == local_seg)[:, None]
        mixed_conv = mixed_conv + jnp.where(
            same_seg, extended[offset : offset + frame_rows] * w_depth[offset], 0.0
        )
    normed_conv = normalize(mixed_conv, depth_gain)
    activated = (normed_conv * jax.nn.sigmoid(normed_conv)).astype(jnp.bfloat16)
    result = (
        residual.astype(jnp.float32)
        + jnp.dot(activated, w_proj, preferred_element_type=jnp.float32)
    ).astype(jnp.bfloat16)
    return result[None]


def solution(mesh):
    in_specs = (P("grp", "blk", None), P(), P(), P(None, "grp"), P(), P(), P(), P(), P(), P())
    out_specs = P("grp", "blk", None)
    return jax.shard_map(body, mesh=mesh, in_specs=in_specs, out_specs=out_specs, check_vma=False)
```

profile of v0, /device:TPU:1, one launch (start us, length us, event | category | flops | bytes accessed | tf_op | source)
XLA Modules:
  0.0 285.7 jit_solution(17601344647619971981)
XLA Ops:
  7.3 1.2 convert_reduce_fusion.1
  8.5 1.3 fusion.39
  9.8 73.4 %all-gather.2.cloned.1.call-done = bf16[1024,3072]{0,1:T(8,128)(2,1)} async-done(((bf16[1024,192]{0,1:T(8,128)(2,1)}), bf16[1024,3072]{0,1:T(8,128)(2,1)}) %all-gather.2.cloned.1.call-update) | async-done | bytes 6291472 | tf_op jit(solution)/shard_map/all_gather | solution.py:57
  83.2 6.0 %convolution_convert_fusion = bf16[256,3072]{1,0:T(8,128)(2,1)} fusion(bf16[1024,3072]{0,1:T(8,128)(2,1)} %all-gather.2.cloned.1.call-done, bf16[1,256,1024]{2,1,0:T(8,128)(2,1)} %param.12, f32[1024]{0:T(1024)} %param.14, f32[256]{0:T(256)S(1)} %add_rsqrt_fusion.2, f32[256]{0:T(256)S(1)} %broadcast_multiply_fusion.2), kind=kOutput, calls=%fused_computation.19 | convolution fusion | flops 1612709888 | bytes 8394752 | tf_op jit(solution)/shard_map/dot_general | solution.py:56
  89.2 2.6 copy.19
  91.8 6.9 %all-to-all-start = ((bf16[256,16,192]{0,2,1:T(8,128)(2,1)}), bf16[256,16,192]{0,2,1:T(8,128)(2,1)}, u32[]{:S(2)}, u32[]{:S(2)}) async-start(bf16[256,16,192]{0,2,1:T(8,128)(2,1)} %bitcast.125), calls=%async_computation | async-start | bytes 3145728 | tf_op jit(solution)/shard_map/all_to_all | solution.py:60
  99.1 35.8 %all-to-all-done = bf16[256,16,192]{0,2,1:T(8,128)(2,1)} async-done(((bf16[256,16,192]{0,2,1:T(8,128)(2,1)}), bf16[256,16,192]{0,2,1:T(8,128)(2,1)}, u32[]{:S(2)}, u32[]{:S(2)}) %all-to-all-start) | async-done | bytes 1572896 | tf_op jit(solution)/shard_map/all_to_all | solution.py:60
  134.8 3.4 %copy.20 = bf16[16,256,192]{1,0,2:T(8,128)(2,1)} copy(bf16[16,256,192]{1,2,0:T(8,128)(2,1)} %bitcast.12) | data formatting | bytes 3145728 | tf_op jit(solution)/shard_map/all_to_all | solution.py:60
  138.3 3.8 %reshape.169 = bf16[4096,1,3,64]{0,3,2,1:T(8,128)(2,1)} reshape(bf16[16,256,192]{1,0,2:T(8,128)(2,1)} %copy.20) | data formatting | bytes 3145728 | tf_op jit(solution)/shard_map/reshape | solution.py:62
  142.0 2.5 slice_bitcast_fusion
  144.5 75.0 %while.10 = (s32[]{:T(128)}, bf16[8,512,64]{1,2,0:T(8,128)(2,1)}, s32[8]{0:T(128)S(1)}, s32[4096]{0:T(1024)S(1)}, bf16[4096,1,64]{0,2,1:T(8,128)(2,1)}, /*index=...) while((s32[]{:T(128)}, bf16[8,512,64]{1,2,0:T(8,128)(2,1)}, ...), condition=%wide.region_7.8_spmd, body=%wide.region_4.0_spmd.sunk | while | flops 566295552 | bytes 26415792 | solution.py:91
  145.8 2.7 fusion.139
  148.5 2.5 fusion.140
  150.9 3.0 %fusion.141 = bf16[8,512,64]{1,2,0:T(8,128)(2,1)} fusion(bf16[8,512,64]{1,2,0:T(8,128)(2,1)} %get-tuple-element.187, s32[]{:T(128)} %get-tuple-element.186, f32[512,4096]{1,0:T(8,128)S(1)} %get-tuple-element.173, f32[512]{0:T(512)S(1)} %get-tuple-element.174, s32[4096]{0:T(1024)S(1)} %get-tuple-element.200, s32[512]{0:T(512)S(1)} %dynamic_slice.21, ...), kind=kOutput, calls=%fused_computation.10.clone.1 | convolution fusion | flops 278986752 | bytes 9001472 | tf_op jit(solution)/shard_map/while/body/eval_jaxpr/hqk,khd->qhd/dot_general | solution.py:82
  155.2 2.6 fusion.139
  157.8 2.5 fusion.140
  160.3 3.0 %fusion.141 = bf16[8,512,64]{1,2,0:T(8,128)(2,1)} fusion(bf16[8,512,64]{1,2,0:T(8,128)(2,1)} %get-tuple-element.187, s32[]{:T(128)} %get-tuple-element.186, f32[512,4096]{1,0:T(8,128)S(1)} %get-tuple-element.173, f32[512]{0:T(512)S(1)} %get-tuple-element.174, s32[4096]{0:T(1024)S(1)} %get-tuple-element.200, s32[512]{0:T(512)S(1)} %dynamic_slice.21, ...), kind=kOutput, calls=%fused_computation.10.clone.1 | convolution fusion | flops 278986752 | bytes 9001472 | tf_op jit(solution)/shard_map/while/body/eval_jaxpr/hqk,khd->qhd/dot_general | solution.py:82
  164.6 2.7 fusion.139
  167.2 2.5 fusion.140
  169.7 3.0 %fusion.141 = bf16[8,512,64]{1,2,0:T(8,128)(2,1)} fusion(bf16[8,512,64]{1,2,0:T(8,128)(2,1)} %get-tuple-element.187, s32[]{:T(128)} %get-tuple-element.186, f32[512,4096]{1,0:T(8,128)S(1)} %get-tuple-element.173, f32[512]{0:T(512)S(1)} %get-tuple-element.174, s32[4096]{0:T(1024)S(1)} %get-tuple-element.200, s32[512]{0:T(512)S(1)} %dynamic_slice.21, ...), kind=kOutput, calls=%fused_computation.10.clone.1 | convolution fusion | flops 278986752 | bytes 9001472 | tf_op jit(solution)/shard_map/while/body/eval_jaxpr/hqk,khd->qhd/dot_general | solution.py:82
  173.9 2.6 fusion.139
  176.6 2.5 fusion.140
  179.1 3.0 %fusion.141 = bf16[8,512,64]{1,2,0:T(8,128)(2,1)} fusion(bf16[8,512,64]{1,2,0:T(8,128)(2,1)} %get-tuple-element.187, s32[]{:T(128)} %get-tuple-element.186, f32[512,4096]{1,0:T(8,128)S(1)} %get-tuple-element.173, f32[512]{0:T(512)S(1)} %get-tuple-element.174, s32[4096]{0:T(1024)S(1)} %get-tuple-element.200, s32[512]{0:T(512)S(1)} %dynamic_slice.21, ...), kind=kOutput, calls=%fused_computation.10.clone.1 | convolution fusion | flops 278986752 | bytes 9001472 | tf_op jit(solution)/shard_map/while/body/eval_jaxpr/hqk,khd->qhd/dot_general | solution.py:82
  183.3 2.7 fusion.139
  186.0 2.5 fusion.140
  188.4 3.0 %fusion.141 = bf16[8,512,64]{1,2,0:T(8,128)(2,1)} fusion(bf16[8,512,64]{1,2,0:T(8,128)(2,1)} %get-tuple-element.187, s32[]{:T(128)} %get-tuple-element.186, f32[512,4096]{1,0:T(8,128)S(1)} %get-tuple-element.173, f32[512]{0:T(512)S(1)} %get-tuple-element.174, s32[4096]{0:T(1024)S(1)} %get-tuple-element.200, s32[512]{0:T(512)S(1)} %dynamic_slice.21, ...), kind=kOutput, calls=%fused_computation.10.clone.1 | convolution fusion | flops 278986752 | bytes 9001472 | tf_op jit(solution)/shard_map/while/body/eval_jaxpr/hqk,khd->qhd/dot_general | solution.py:82
  192.7 2.6 fusion.139
  195.4 2.5 fusion.140
  197.8 3.0 %fusion.141 = bf16[8,512,64]{1,2,0:T(8,128)(2,1)} fusion(bf16[8,512,64]{1,2,0:T(8,128)(2,1)} %get-tuple-element.187, s32[]{:T(128)} %get-tuple-element.186, f32[512,4096]{1,0:T(8,128)S(1)} %get-tuple-element.173, f32[512]{0:T(512)S(1)} %get-tuple-element.174, s32[4096]{0:T(1024)S(1)} %get-tuple-element.200, s32[512]{0:T(512)S(1)} %dynamic_slice.21, ...), kind=kOutput, calls=%fused_computation.10.clone.1 | convolution fusion | flops 278986752 | bytes 9001472 | tf_op jit(solution)/shard_map/while/body/eval_jaxpr/hqk,khd->qhd/dot_general | solution.py:82
  202.1 2.7 fusion.139
  204.7 2.5 fusion.140
  207.2 3.0 %fusion.141 = bf16[8,512,64]{1,2,0:T(8,128)(2,1)} fusion(bf16[8,512,64]{1,2,0:T(8,128)(2,1)} %get-tuple-element.187, s32[]{:T(128)} %get-tuple-element.186, f32[512,4096]{1,0:T(8,128)S(1)} %get-tuple-element.173, f32[512]{0:T(512)S(1)} %get-tuple-element.174, s32[4096]{0:T(1024)S(1)} %get-tuple-element.200, s32[512]{0:T(512)S(1)} %dynamic_slice.21, ...), kind=kOutput, calls=%fused_computation.10.clone.1 | convolution fusion | flops 278986752 | bytes 9001472 | tf_op jit(solution)/shard_map/while/body/eval_jaxpr/hqk,khd->qhd/dot_general | solution.py:82
  211.5 2.6 fusion.139
  214.1 2.5 fusion.140
  216.6 3.0 %fusion.141 = bf16[8,512,64]{1,2,0:T(8,128)(2,1)} fusion(bf16[8,512,64]{1,2,0:T(8,128)(2,1)} %get-tuple-element.187, s32[]{:T(128)} %get-tuple-element.186, f32[512,4096]{1,0:T(8,128)S(1)} %get-tuple-element.173, f32[512]{0:T(512)S(1)} %get-tuple-element.174, s32[4096]{0:T(1024)S(1)} %get-tuple-element.200, s32[512]{0:T(512)S(1)} %dynamic_slice.21, ...), kind=kOutput, calls=%fused_computation.10.clone.1 | convolution fusion | flops 278986752 | bytes 9001472 | tf_op jit(solution)/shard_map/while/body/eval_jaxpr/hqk,khd->qhd/dot_general | solution.py:82
  219.6 1.4 copy.21
  221.9 2.0 copy.22
  223.9 6.8 %all-to-all-start.1 = ((bf16[16,256,64]{1,2,0:T(8,128)(2,1)}), bf16[16,256,64]{1,2,0:T(8,128)(2,1)S(1)}, u32[]{:S(2)}, u32[]{:S(2)}) async-start(bf16[16,256,64]{1,2,0:T(8,128)(2,1)} %copy.22), calls=%async_computation.1 | async-start | bytes 1048576 | tf_op jit(solution)/shard_map/all_to_all | solution.py:93
  231.1 15.4 %all-to-all-done.1 = bf16[16,256,64]{1,2,0:T(8,128)(2,1)S(1)} async-done(((bf16[16,256,64]{1,2,0:T(8,128)(2,1)}), bf16[16,256,64]{1,2,0:T(8,128)(2,1)S(1)}, u32[]{:S(2)}, u32[]{:S(2)}) %all-to-all-start.1) | async-done | bytes 524320 | tf_op jit(solution)/shard_map/all_to_all | solution.py:93
  247.3 1.9 fusion.29
  249.7 1.4 fusion.109
  251.8 3.6 %collective-permute-start.2 = (bf16[15,1024]{1,0:T(8,128)(2,1)S(1)}, bf16[15,1024]{1,0:T(8,128)(2,1)S(1)}, u32[]{:S(2)}, u32[]{:S(2)}) collective-permute-start(bf16[15,1024]{1,0:T(8,128)(2,1)S(1)} %get-tuple-element.65), channel_id=1, source_target_pairs={{16,0},{32,16},{48,32},{64,48},{80,64},{96,80},{112,96},{128,112},... | collective-permute-start | bytes 92168 | tf_op jit(solution)/shard_map/ppermute | solution.py:21
  255.4 1.1 collective-permute-done
  256.5 7.0 %collective-permute-start.1 = (bf16[1,15,1024]{2,1,0:T(8,128)(2,1)S(1)}, bf16[1,15,1024]{2,1,0:T(8,128)(2,1)S(1)}, u32[]{:S(2)}, u32[]{:S(2)}) collective-permute-start(bf16[1,15,1024]{2,1,0:T(8,128)(2,1)S(1)} %bitcast.127), channel_id=1, source_target_pairs={{0,1},{1,2},{2,3},{3,4},{4,5},{5,6},{6,7},{7,8},{8,9},{9,10},{10,1... | collective-permute-start | bytes 92168 | tf_op jit(solution)/shard_map/ppermute | solution.py:18
  263.7 1.9 collective-permute-start.3
  265.6 4.8 %collective-permute-done.3 = bf16[1,15,1024]{2,1,0:T(8,128)(2,1)S(1)} collective-permute-done((bf16[1,15,1024]{2,1,0:T(8,128)(2,1)S(1)}, bf16[1,15,1024]{2,1,0:T(8,128)(2,1)S(1)}, u32[]{:S(2)}, u32[]{:S(2)}) %collective-permute-start.3) | collective-permute-done | bytes 30752 | tf_op jit(solution)/shard_map/ppermute | solution.py:21
  270.6 6.3 %fusion.122 = (f32[256]{0:T(256)S(1)}, f32[256,1024]{1,0:T(8,128)S(1)}) fusion(f32[1024]{0:T(1024)S(1)} %bitcast.139, f32[286,1024]{1,0:T(8,128)S(1)} %maximum_convert_fusion, pred[256]{0:T(512)(128)(4,1)S(1)} %get-tuple-element.98, f32[1024]{0:T(1024)S(1)} %bitcast.140, pred[256]{0:T(512)(128)(4,1)S(1)} %get-tuple-element.99, f32[1024]{0:T(1024)S(1)} %bitcast.142, ...), kind=kLoop, calls=%fused_computation.205 | loop fusion | flops 24379136 | bytes 33690368 | tf_op jit(solution)/shard_map/reduce_sum | solution.py:27
  277.1 1.7 fusion.35
  (70 shorter events, 10.1 us)
Async XLA Ops:
  6.5 240.7 %copy-start = (bf16[1024,1024]{1,0:T(8,128)(2,1)S(1)}, bf16[1024,1024]{1,0:T(8,128)(2,1)}, u32[]{:S(2)}) copy-start(bf16[1024,1024]{1,0:T(8,128)(2,1)} %param.16) | copy-start | bytes 6291460
  6.5 76.6 %all-gather.2.cloned.1.call-start = ((), (), s32[]{:S(2)}) async-start(), calls=%async_computation.2 | async-start | bytes 6684672 | tf_op jit(solution)/shard_map/all_gather | solution.py:57
  89.2 9.5 %copy-start.8 = (s32[8]{0:T(128)S(1)}, s32[8]{0:T(128)}, u32[]{:S(2)}) copy-start(s32[8]{0:T(128)} %param.13) | copy-start | bytes 100
  91.8 43.0 %all-to-all-start = ((bf16[256,16,192]{0,2,1:T(8,128)(2,1)}), bf16[256,16,192]{0,2,1:T(8,128)(2,1)}, u32[]{:S(2)}, u32[]{:S(2)}) async-start(bf16[256,16,192]{0,2,1:T(8,128)(2,1)} %bitcast.125), calls=%async_computation | async-start | bytes 3145728 | tf_op jit(solution)/shard_map/all_to_all | solution.py:60
  219.5 11.4 %copy-start.3 = (f32[31,1024]{1,0:T(8,128)S(1)}, f32[31,1024]{1,0:T(8,128)}, u32[]{:S(2)}) copy-start(f32[31,1024]{1,0:T(8,128)} %param.19) | copy-start | bytes 380932
  219.5 27.7 %copy-start.1 = (bf16[1,256,1024]{2,1,0:T(8,128)(2,1)S(1)}, bf16[1,256,1024]{2,1,0:T(8,128)(2,1)}, u32[]{:S(2)}) copy-start(bf16[1,256,1024]{2,1,0:T(8,128)(2,1)} %param.12) | copy-start | bytes 1572868
  221.0 28.7 %copy-start.6 = (f32[1024]{0:T(1024)S(1)}, f32[1024]{0:T(1024)}, u32[]{:S(2)}) copy-start(f32[1024]{0:T(1024)} %param.17) | copy-start | bytes 12292
  223.9 22.6 %all-to-all-start.1 = ((bf16[16,256,64]{1,2,0:T(8,128)(2,1)}), bf16[16,256,64]{1,2,0:T(8,128)(2,1)S(1)}, u32[]{:S(2)}, u32[]{:S(2)}) async-start(bf16[16,256,64]{1,2,0:T(8,128)(2,1)} %copy.22), calls=%async_computation.1 | async-start | bytes 1048576 | tf_op jit(solution)/shard_map/all_to_all | solution.py:93
  246.5 0.8 copy-start.2
  247.3 2.4 copy-start.4
  251.4 5.1 %collective-permute-start = (bf16[15,1024]{1,0:T(8,128)(2,1)S(1)}, bf16[15,1024]{1,0:T(8,128)(2,1)S(1)}, u32[]{:S(2)}, u32[]{:S(2)}) collective-permute-start(bf16[15,1024]{1,0:T(8,128)(2,1)S(1)} %get-tuple-element.64), channel_id=1, source_target_pairs={{0,16},{16,32},{32,48},{48,64},{64,80},{80,96},{96,112},{112,128},... | collective-permute-start | bytes 92168 | tf_op jit(solution)/shard_map/ppermute | solution.py:18
  251.8 11.8 %collective-permute-start.2 = (bf16[15,1024]{1,0:T(8,128)(2,1)S(1)}, bf16[15,1024]{1,0:T(8,128)(2,1)S(1)}, u32[]{:S(2)}, u32[]{:S(2)}) collective-permute-start(bf16[15,1024]{1,0:T(8,128)(2,1)S(1)} %get-tuple-element.65), channel_id=1, source_target_pairs={{16,0},{32,16},{48,32},{64,48},{80,64},{96,80},{112,96},{128,112},... | collective-permute-start | bytes 92168 | tf_op jit(solution)/shard_map/ppermute | solution.py:21
  256.5 9.1 %collective-permute-start.1 = (bf16[1,15,1024]{2,1,0:T(8,128)(2,1)S(1)}, bf16[1,15,1024]{2,1,0:T(8,128)(2,1)S(1)}, u32[]{:S(2)}, u32[]{:S(2)}) collective-permute-start(bf16[1,15,1024]{2,1,0:T(8,128)(2,1)S(1)} %bitcast.127), channel_id=1, source_target_pairs={{0,1},{1,2},{2,3},{3,4},{4,5},{5,6},{6,7},{7,8},{8,9},{9,10},{10,1... | collective-permute-start | bytes 92168 | tf_op jit(solution)/shard_map/ppermute | solution.py:18
  263.7 6.7 %collective-permute-start.3 = (bf16[1,15,1024]{2,1,0:T(8,128)(2,1)S(1)}, bf16[1,15,1024]{2,1,0:T(8,128)(2,1)S(1)}, u32[]{:S(2)}, u32[]{:S(2)}) collective-permute-start(bf16[1,15,1024]{2,1,0:T(8,128)(2,1)S(1)} %bitcast.128), channel_id=1, source_target_pairs={{1,0},{2,1},{3,2},{4,3},{5,4},{6,5},{7,6},{8,7},{9,8},{10,9},{11,1... | collective-permute-start | bytes 92168 | tf_op jit(solution)/shard_map/ppermute | solution.py:21
  270.6 6.6 %copy-start.5 = (bf16[1024,1024]{1,0:T(8,128)(2,1)S(1)}, bf16[1024,1024]{1,0:T(8,128)(2,1)}, u32[]{:S(2)}) copy-start(bf16[1024,1024]{1,0:T(8,128)(2,1)} %param.21) | copy-start | bytes 6291460
  270.6 6.6 %copy-start.7 = (f32[1024]{0:T(1024)S(1)}, f32[1024]{0:T(1024)}, u32[]{:S(2)}) copy-start(f32[1024]{0:T(1024)} %param.20) | copy-start | bytes 12292
Sparse Core Ops, SparseCore 0:
  10.0 73.0 all-gather.1
where the time goes:
time: 287 us; the launch traced here: 286 us
  waiting for transfers between devices  131 us (46%)
  matrix products  55.9 us (19%)
  other arithmetic  30.3 us (11%)
  starting transfers between devices  26.6 us (9%)
  local copies, waits for them, and re-layouts  22.9 us (8%)
  between operations  13.7 us (5%)
  loops' own time  5.04 us (2%)
    all_gather x1, waiting for transfers between devices, body(): lax.all_gather(w_qkv, 'grp', axis=1, tiled=True)  73.4 us
    all_to_all x1, waiting for transfers between devices, body(): lax.all_to_all(qkv_rows, 'blk', split_axis=1, concat_axis=0, tiled=True)  35.8 us
    dot_general x8, matrix products, attend(): jnp.einsum('hqk,khd->qhd', weights.astype(jnp.bfloat16), values_all, pref...  23.7 us
    dot_general x8, matrix products, attend(): jnp.einsum('qhd,khd->hqk', queries, keys_all, preferred_element_type=jnp....  21.2 us
    reduce_sum x8, other arithmetic, attend(): row_total = jnp.sum(weights, axis=2)  19.8 us
    all_to_all x1, waiting for transfers between devices, body(): lax.all_to_all(merged_heads, 'blk', split_axis=0, concat_axis=1, tiled=True)  15.4 us
    reduce_sum x3, other arithmetic, normalize(): center = values - jnp.mean(values, axis=-1, keepdims=True)  7.59 us
    ppermute x2, starting transfers between devices, padded_2(): lax.ppermute(lax.slice_in_dim(block, block.shape[dim] - width, None, axis...  7.35 us
  transfers between devices with their start and end apart: 7, of which 5 were waited for; matrix products, arithmetic and copies ran while one was open for 1% of the time, Pallas kernels for 0%

commit v1 on v0

--- a/solution.py
+++ b/solution.py
@@ -54,7 +54,11 @@
     local_float = local_frames.astype(jnp.float32)
     normed = normalize(local_float, attn_gain).astype(jnp.bfloat16)
     qkv_rows = jnp.dot(
-        normed, lax.all_gather(w_qkv, "grp", axis=1, tiled=True), preferred_element_type=jnp.float32
+        normed,
+        jnp.concatenate(
+            lax.all_to_all(jnp.stack([w_qkv] * lax.axis_size("grp")), "grp", 0, 0), axis=1
+        ),
+        preferred_element_type=jnp.float32,
     ).astype(jnp.bfloat16)
     local_seg = segment_of(utt_lengths, first_frame + jnp.arange(frame_rows, dtype=jnp.int32))
     my_heads = lax.all_to_all(qkv_rows, "blk", split_axis=1, concat_axis=0, tiled=True)

time: 287 us -> 307 us (1.070)
  the two profiles are of different devices: /device:TPU:1 before, /device:TPU:5 now
where the time goes in v1:
time: 307 us; the launch traced here: 306 us
  waiting for transfers between devices  140 us (46%)
  starting transfers between devices  52.5 us (17%)
  matrix products  50.8 us (17%)
  local copies, waits for them, and re-layouts  28.4 us (9%)
  other arithmetic  28.3 us (9%)
  loops' own time  5.32 us (2%)
    all_to_all x1, waiting for transfers between devices, body(): lax.all_to_all(jnp.stack([w_qkv] * lax.axis_size('grp')), 'grp', 0, 0)  83.3 us
    all_to_all x1, waiting for transfers between devices, body(): lax.all_to_all(qkv_rows, 'blk', split_axis=1, concat_axis=0, tiled=True)  35.7 us
    ppermute x2, starting transfers between devices, padded_2(): lax.ppermute(lax.slice_in_dim(block, block.shape[dim] - width, None, axis...  23.8 us
    dot_general x8, matrix products, attend(): jnp.einsum('qhd,khd->hqk', queries, keys_all, preferred_element_type=jnp....  21.2 us
    reduce_sum x8, other arithmetic, attend(): row_total = jnp.sum(weights, axis=2)  19.8 us
    dot_general x8, matrix products, attend(): jnp.einsum('hqk,khd->qhd', weights.astype(jnp.bfloat16), values_all, pref...  18.8 us
    all_to_all x1, waiting for transfers between devices, body(): lax.all_to_all(merged_heads, 'blk', split_axis=0, concat_axis=1, tiled=True)  15.5 us
    all_to_all x1, starting transfers between devices, body(): lax.all_to_all(qkv_rows, 'blk', split_axis=1, concat_axis=0, tiled=True)  8.45 us
  transfers between devices with their start and end apart: 7, of which 5 were waited for; matrix products, arithmetic and copies ran while one was open for 0% of the time, Pallas kernels for 0%

profile of v1, /device:TPU:5, one launch (start us, length us, event | category | flops | bytes accessed | tf_op | source)
XLA Modules:
  0.0 306.1 jit_solution(15594959586024860666)
XLA Ops:
  0.0 4.6 %stack.6 = bf16[16,1024,192]{1,2,0:T(8,128)(2,1)} broadcast(bf16[1024,192]{0,1:T(8,128)(2,1)} %param.15), dimensions={1,2} | broadcast | bytes 6684672 | tf_op jit(solution)/shard_map/stack | solution.py:59
  4.6 7.9 %all-to-all-start = ((bf16[16,1024,192]{1,2,0:T(8,128)(2,1)}), bf16[16,1024,192]{1,2,0:T(8,128)(2,1)}, u32[]{:S(2)}, u32[]{:S(2)}) async-start(bf16[16,1024,192]{1,2,0:T(8,128)(2,1)} %stack.6), calls=%async_computation | async-start | bytes 12582912 | tf_op jit(solution)/shard_map/all_to_all | solution.py:59
  12.9 83.3 %all-to-all-done = bf16[16,1024,192]{1,2,0:T(8,128)(2,1)} async-done(((bf16[16,1024,192]{1,2,0:T(8,128)(2,1)}), bf16[16,1024,192]{1,2,0:T(8,128)(2,1)}, u32[]{:S(2)}, u32[]{:S(2)}) %all-to-all-start) | async-done | bytes 6291488 | tf_op jit(solution)/shard_map/all_to_all | solution.py:59
  96.3 5.8 %convolution_convert_fusion = bf16[256,3072]{1,0:T(8,128)(2,1)} fusion(bf16[1024,3072]{0,1:T(8,128)(2,1)} %bitcast.13, bf16[1,256,1024]{2,1,0:T(8,128)(2,1)S(1)} %copy-done.1, f32[1024]{0:T(1024)S(1)} %copy-done.8, f32[256]{0:T(256)S(1)} %add_rsqrt_fusion.2, f32[256]{0:T(256)S(1)} %broadcast_multiply_fusion.2), kind=kOutput, calls=%fused_computation.19 | convolution fusion | flops 1612709888 | bytes 8394752 | tf_op jit(solution)/shard_map/dot_general | solution.py:56
  102.1 2.6 copy.20
  104.7 8.4 %all-to-all-start.1 = ((bf16[256,16,192]{0,2,1:T(8,128)(2,1)}), bf16[256,16,192]{0,2,1:T(8,128)(2,1)}, u32[]{:S(2)}, u32[]{:S(2)}) async-start(bf16[256,16,192]{0,2,1:T(8,128)(2,1)} %bitcast.124), calls=%async_computation.1 | async-start | bytes 3145728 | tf_op jit(solution)/shard_map/all_to_all | solution.py:64
  113.5 35.7 %all-to-all-done.1 = bf16[256,16,192]{0,2,1:T(8,128)(2,1)} async-done(((bf16[256,16,192]{0,2,1:T(8,128)(2,1)}), bf16[256,16,192]{0,2,1:T(8,128)(2,1)}, u32[]{:S(2)}, u32[]{:S(2)}) %all-to-all-start.1) | async-done | bytes 1572896 | tf_op jit(solution)/shard_map/all_to_all | solution.py:64
  149.2 3.4 %copy.21 = bf16[16,256,192]{1,0,2:T(8,128)(2,1)} copy(bf16[16,256,192]{1,2,0:T(8,128)(2,1)} %bitcast.15) | data formatting | bytes 3145728 | tf_op jit(solution)/shard_map/all_to_all | solution.py:64
  152.6 3.8 %reshape.200 = bf16[4096,1,3,64]{0,3,2,1:T(8,128)(2,1)} reshape(bf16[16,256,192]{1,0,2:T(8,128)(2,1)} %copy.21) | data formatting | bytes 3145728 | tf_op jit(solution)/shard_map/reshape | solution.py:66
  156.4 2.5 slice_bitcast_fusion
  158.9 70.5 %while.10 = (s32[]{:T(128)}, bf16[8,512,64]{1,2,0:T(8,128)(2,1)S(1)}, s32[8]{0:T(128)S(1)}, s32[4096]{0:T(1024)S(1)}, bf16[4096,1,64]{0,2,1:T(8,128)(2,1)}, /*in...) while((s32[]{:T(128)}, ...), condition=%wide.region_7.8_spmd, body=%wide.region_4.0_spmd.sunk | while | flops 566295552 | bytes 28512464 | solution.py:95
  160.2 2.6 fusion.140
  162.9 2.5 fusion.141
  165.4 2.3 fusion.142
  169.0 2.7 fusion.140
  171.7 2.5 fusion.141
  174.2 2.3 fusion.142
  177.9 2.7 fusion.140
  180.5 2.5 fusion.141
  183.0 2.3 fusion.142
  186.7 2.7 fusion.140
  189.3 2.5 fusion.141
  191.8 2.3 fusion.142
  195.5 2.7 fusion.140
  198.2 2.5 fusion.141
  200.6 2.3 fusion.142
  204.3 2.7 fusion.140
  207.0 2.5 fusion.141
  209.5 2.3 fusion.142
  213.1 2.7 fusion.140
  215.8 2.5 fusion.141
  218.3 2.3 fusion.142
  221.9 2.7 fusion.140
  224.6 2.5 fusion.141
  227.1 2.3 fusion.142
  230.3 1.4 copy.22
  232.6 2.0 copy.23
  234.6 6.9 %all-to-all-start.2 = ((bf16[16,256,64]{1,2,0:T(8,128)(2,1)}), bf16[16,256,64]{1,2,0:T(8,128)(2,1)S(1)}, u32[]{:S(2)}, u32[]{:S(2)}) async-start(bf16[16,256,64]{1,2,0:T(8,128)(2,1)} %copy.23), calls=%async_computation.2 | async-start | bytes 1048576 | tf_op jit(solution)/shard_map/all_to_all | solution.py:97
  241.8 15.5 %all-to-all-done.2 = bf16[16,256,64]{1,2,0:T(8,128)(2,1)S(1)} async-done(((bf16[16,256,64]{1,2,0:T(8,128)(2,1)}), bf16[16,256,64]{1,2,0:T(8,128)(2,1)S(1)}, u32[]{:S(2)}, u32[]{:S(2)}) %all-to-all-start.2) | async-done | bytes 524320 | tf_op jit(solution)/shard_map/all_to_all | solution.py:97
  258.1 1.9 fusion.29
  260.5 1.4 fusion.110
  262.4 3.6 %collective-permute-start.2 = (bf16[15,1024]{1,0:T(8,128)(2,1)S(1)}, bf16[15,1024]{1,0:T(8,128)(2,1)S(1)}, u32[]{:S(2)}, u32[]{:S(2)}) collective-permute-start(bf16[15,1024]{1,0:T(8,128)(2,1)S(1)} %get-tuple-element.65), channel_id=1, source_target_pairs={{16,0},{32,16},{48,32},{64,48},{80,64},{96,80},{112,96},{128,112},... | collective-permute-start | bytes 92168 | tf_op jit(solution)/shard_map/ppermute | solution.py:21
  266.0 1.1 collective-permute-done
  267.2 23.6 %collective-permute-start.1 = (bf16[1,15,1024]{2,1,0:T(8,128)(2,1)S(1)}, bf16[1,15,1024]{2,1,0:T(8,128)(2,1)S(1)}, u32[]{:S(2)}, u32[]{:S(2)}) collective-permute-start(bf16[1,15,1024]{2,1,0:T(8,128)(2,1)S(1)} %bitcast.126), channel_id=1, source_target_pairs={{0,1},{1,2},{2,3},{3,4},{4,5},{5,6},{6,7},{7,8},{8,9},{9,10},{10,1... | collective-permute-start | bytes 92168 | tf_op jit(solution)/shard_map/ppermute | solution.py:18
  290.9 1.9 collective-permute-start.3
  292.9 4.8 %collective-permute-done.3 = bf16[1,15,1024]{2,1,0:T(8,128)(2,1)S(1)} collective-permute-done((bf16[1,15,1024]{2,1,0:T(8,128)(2,1)S(1)}, bf16[1,15,1024]{2,1,0:T(8,128)(2,1)S(1)}, u32[]{:S(2)}, u32[]{:S(2)}) %collective-permute-start.3) | collective-permute-done | bytes 30752 | tf_op jit(solution)/shard_map/ppermute | solution.py:21
  297.8 6.3 %fusion.123 = (f32[256]{0:T(256)S(1)}, f32[256,1024]{1,0:T(8,128)S(1)}) fusion(f32[1024]{0:T(1024)S(1)} %bitcast.138, f32[286,1024]{1,0:T(8,128)S(1)} %maximum_convert_fusion, pred[256]{0:T(512)(128)(4,1)S(1)} %get-tuple-element.98, f32[1024]{0:T(1024)S(1)} %bitcast.139, pred[256]{0:T(512)(128)(4,1)S(1)} %get-tuple-element.99, f32[1024]{0:T(1024)S(1)} %bitcast.141, ...), kind=kLoop, calls=%fused_computation.207 | loop fusion | flops 24379136 | bytes 33690368 | tf_op jit(solution)/shard_map/reduce_sum | solution.py:27
  304.4 1.7 fusion.33
  (90 shorter events, 10.5 us)
Async XLA Ops:
  0.0 258.1 %copy-start = (bf16[1024,1024]{1,0:T(8,128)(2,1)S(1)}, bf16[1024,1024]{1,0:T(8,128)(2,1)}, u32[]{:S(2)}) copy-start(bf16[1024,1024]{1,0:T(8,128)(2,1)} %param.16) | copy-start | bytes 6291460
  4.6 7.9 %copy-start.1 = (bf16[1,256,1024]{2,1,0:T(8,128)(2,1)S(1)}, bf16[1,256,1024]{2,1,0:T(8,128)(2,1)}, u32[]{:S(2)}) copy-start(bf16[1,256,1024]{2,1,0:T(8,128)(2,1)} %param.12) | copy-start | bytes 1572868
  4.6 91.7 %copy-start.8 = (f32[1024]{0:T(1024)S(1)}, f32[1024]{0:T(1024)}, u32[]{:S(2)}) copy-start(f32[1024]{0:T(1024)} %param.14) | copy-start | bytes 12292
  4.6 91.7 %all-to-all-start = ((bf16[16,1024,192]{1,2,0:T(8,128)(2,1)}), bf16[16,1024,192]{1,2,0:T(8,128)(2,1)}, u32[]{:S(2)}, u32[]{:S(2)}) async-start(bf16[16,1024,192]{1,2,0:T(8,128)(2,1)} %stack.6), calls=%async_computation | async-start | bytes 12582912 | tf_op jit(solution)/shard_map/all_to_all | solution.py:59
  102.1 11.1 %copy-start.11 = (s32[8]{0:T(128)S(1)}, s32[8]{0:T(128)}, u32[]{:S(2)}) copy-start(s32[8]{0:T(128)} %param.13) | copy-start | bytes 100
  104.7 44.5 %all-to-all-start.1 = ((bf16[256,16,192]{0,2,1:T(8,128)(2,1)}), bf16[256,16,192]{0,2,1:T(8,128)(2,1)}, u32[]{:S(2)}, u32[]{:S(2)}) async-start(bf16[256,16,192]{0,2,1:T(8,128)(2,1)} %bitcast.124), calls=%async_computation.1 | async-start | bytes 3145728 | tf_op jit(solution)/shard_map/all_to_all | solution.py:64
  162.9 2.5 copy-start.4
  171.7 2.5 copy-start.4
  180.5 2.5 copy-start.4
  189.3 2.5 copy-start.4
  198.1 2.5 copy-start.4
  207.0 2.5 copy-start.4
  215.8 2.5 copy-start.4
  224.6 2.5 copy-start.4
  229.5 0.8 copy-start.3
  230.2 11.5 %copy-start.5 = (f32[31,1024]{1,0:T(8,128)S(1)}, f32[31,1024]{1,0:T(8,128)}, u32[]{:S(2)}) copy-start(f32[31,1024]{1,0:T(8,128)} %param.19) | copy-start | bytes 380932
  231.6 28.9 %copy-start.9 = (f32[1024]{0:T(1024)S(1)}, f32[1024]{0:T(1024)}, u32[]{:S(2)}) copy-start(f32[1024]{0:T(1024)} %param.17) | copy-start | bytes 12292
  234.6 22.7 %all-to-all-start.2 = ((bf16[16,256,64]{1,2,0:T(8,128)(2,1)}), bf16[16,256,64]{1,2,0:T(8,128)(2,1)S(1)}, u32[]{:S(2)}, u32[]{:S(2)}) async-start(bf16[16,256,64]{1,2,0:T(8,128)(2,1)} %copy.23), calls=%async_computation.2 | async-start | bytes 1048576 | tf_op jit(solution)/shard_map/all_to_all | solution.py:97
  257.3 0.8 copy-start.2
  258.1 2.4 copy-start.6
  262.2 5.0 %collective-permute-start = (bf16[15,1024]{1,0:T(8,128)(2,1)S(1)}, bf16[15,1024]{1,0:T(8,128)(2,1)S(1)}, u32[]{:S(2)}, u32[]{:S(2)}) collective-permute-start(bf16[15,1024]{1,0:T(8,128)(2,1)S(1)} %get-tuple-element.64), channel_id=1, source_target_pairs={{0,16},{16,32},{32,48},{48,64},{64,80},{80,96},{96,112},{112,128},... | collective-permute-start | bytes 92168 | tf_op jit(solution)/shard_map/ppermute | solution.py:18
  262.4 28.5 %collective-permute-start.2 = (bf16[15,1024]{1,0:T(8,128)(2,1)S(1)}, bf16[15,1024]{1,0:T(8,128)(2,1)S(1)}, u32[]{:S(2)}, u32[]{:S(2)}) collective-permute-start(bf16[15,1024]{1,0:T(8,128)(2,1)S(1)} %get-tuple-element.65), channel_id=1, source_target_pairs={{16,0},{32,16},{48,32},{64,48},{80,64},{96,80},{112,96},{128,112},... | collective-permute-start | bytes 92168 | tf_op jit(solution)/shard_map/ppermute | solution.py:21
  267.2 25.7 %collective-permute-start.1 = (bf16[1,15,1024]{2,1,0:T(8,128)(2,1)S(1)}, bf16[1,15,1024]{2,1,0:T(8,128)(2,1)S(1)}, u32[]{:S(2)}, u32[]{:S(2)}) collective-permute-start(bf16[1,15,1024]{2,1,0:T(8,128)(2,1)S(1)} %bitcast.126), channel_id=1, source_target_pairs={{0,1},{1,2},{2,3},{3,4},{4,5},{5,6},{6,7},{7,8},{8,9},{9,10},{10,1... | collective-permute-start | bytes 92168 | tf_op jit(solution)/shard_map/ppermute | solution.py:18
  290.9 6.7 %collective-permute-start.3 = (bf16[1,15,1024]{2,1,0:T(8,128)(2,1)S(1)}, bf16[1,15,1024]{2,1,0:T(8,128)(2,1)S(1)}, u32[]{:S(2)}, u32[]{:S(2)}) collective-permute-start(bf16[1,15,1024]{2,1,0:T(8,128)(2,1)S(1)} %bitcast.127), channel_id=1, source_target_pairs={{1,0},{2,1},{3,2},{4,3},{5,4},{6,5},{7,6},{8,7},{9,8},{10,9},{11,1... | collective-permute-start | bytes 92168 | tf_op jit(solution)/shard_map/ppermute | solution.py:21
  297.8 6.6 %copy-start.7 = (bf16[1024,1024]{1,0:T(8,128)(2,1)S(1)}, bf16[1024,1024]{1,0:T(8,128)(2,1)}, u32[]{:S(2)}) copy-start(bf16[1024,1024]{1,0:T(8,128)(2,1)} %param.21) | copy-start | bytes 6291460
  297.8 6.6 %copy-start.10 = (f32[1024]{0:T(1024)S(1)}, f32[1024]{0:T(1024)}, u32[]{:S(2)}) copy-start(f32[1024]{0:T(1024)} %param.20) | copy-start | bytes 12292
